TPU v7x, 128 devices: a whole 4x4x4 slice. The times are simulated.
128 devices in a mesh: grp: 8 (over x, core), dev: 16 (over y, z).
Axes of the slice: x: 4, y: 4, z: 4, core: 2. Of those that a mesh axis runs over, the one named last changes fastest.
Arguments:
- sep_inv: bfloat16 [4096, 4096], P('grp', 'dev'), may hold values from -0.125 to 0.125
- panels: bfloat16 [8, 96, 2048, 128], P('grp', 'dev'), may hold values from -1.1953125 to 1.1953125
- diag_inverse: bfloat16 [8, 96, 768, 128], P('grp', 'dev'), may hold values from -6 to 6
- widths: int32 [8, 32], P('grp'), may hold values from 1 to 6, 96 in all within a row
- ancestors: int32 [8, 32, 16], P('grp'), may hold values from 0 to 31, as said below
Outputs:
- off_diag: bfloat16 [8, 96, 2048, 128], P('grp', 'dev')
- diag_panels: bfloat16 [8, 96, 768, 128], P('grp', 'dev')
Inputs may be any that keep to these rules, and one draw needn't show every extreme that they name: `widths`: each row of a subtree sums to 96. `ancestors`: each supernode's list holds 16 different separator tile numbers in increasing order.
All inputs are finite; a program needn't handle non-finite values.
Results may differ from a plain program's by a relative error of at most 0.0046.
Values may be sent and summed in bfloat16 or wider, within the bound.
No kernel may reach another device: no remote copies, remote signals or barrier semaphores. Data moves between devices by JAX's collectives and lax.ppermute only.
A program may use at most 320 MiB of HBM per device.

v0:
```python
import jax
import jax.numpy as jnp
from jax import lax
from jax.sharding import PartitionSpec as P


def extended_2(cells, sides, width):
    for axis, dim in sides:
        count = lax.axis_size(axis)
        ends = count - 1
        head = lax.slice_in_dim(cells, 0, width, axis=dim)
        tail = lax.slice_in_dim(cells, cells.shape[dim] - width, cells.shape[dim], axis=dim)
        cells = jnp.concatenate(
            [
                lax.ppermute(tail, axis, [(i, (i + 1) % count) for i in range(ends)]),
                cells,
                lax.ppermute(head, axis, [((i + 1) % count, i) for i in range(ends)]),
            ],
            axis=dim,
        )
    return cells


def on_device(sep_inv, panels, diag_inverse, widths, ancestors):
    group_count = lax.axis_size("grp")
    device_count = lax.axis_size("dev")
    rows_local = sep_inv.shape[0]
    cols_local = sep_inv.shape[1]
    stacked = lax.all_gather(sep_inv[None], ("grp", "dev"), axis=0, tiled=True)
    whole_sep = stacked.reshape(group_count, device_count, rows_local, cols_local)
    whole_sep = whole_sep.transpose(0, 2, 1, 3).reshape(
        group_count * rows_local, device_count * cols_local
    )
    block = panels.shape[3]
    anc_rows = panels.shape[2]
    anc_tiles = anc_rows // block
    local_units = panels.shape[1]
    max_tiles = diag_inverse.shape[2] // block
    sep_order = whole_sep.shape[0]
    count_blocks = sep_order // block
    row_tiles = whole_sep.reshape(count_blocks, block, sep_order)
    extended = extended_2(panels, (("dev", 1),), max_tiles - 1)
    width_row = widths[0]
    anc_table = ancestors[0]
    supernodes = width_row.shape[0]
    ends = jnp.cumsum(width_row)
    starts = ends - width_row
    position = lax.axis_index("dev") * local_units + jnp.arange(local_units, dtype=jnp.int32)
    owner = jnp.sum((ends[None, :] <= position[:, None]).astype(jnp.int32), axis=1)
    one_hot = (jnp.arange(supernodes, dtype=jnp.int32)[None, :] == owner[:, None]).astype(jnp.int32)
    column = position - jnp.sum(one_hot * starts[None, :], axis=1)
    width_unit = jnp.sum(one_hot * width_row[None, :], axis=1)
    blocks = jnp.sum(one_hot[:, :, None] * anc_table[None, :, :], axis=1)
    tile_ids = jnp.arange(count_blocks, dtype=jnp.int32)

    def per_unit(unit_idx):
        chosen = blocks[unit_idx]
        rows_pick = jnp.take(row_tiles, chosen, axis=0).reshape(anc_rows, sep_order)
        placing = (tile_ids[:, None] == chosen[None, :]).astype(jnp.bfloat16)
        panel_flat = panels[0, unit_idx].reshape(anc_tiles, block * block)
        spread = jnp.dot(placing, panel_flat, preferred_element_type=jnp.float32)
        spread = spread.astype(jnp.bfloat16).reshape(sep_order, block)
        product = jnp.dot(rows_pick, spread, preferred_element_type=jnp.float32)
        result_x = (-product).astype(jnp.bfloat16)
        start_at = unit_idx + max_tiles - 1 - column[unit_idx]
        related = lax.dynamic_slice_in_dim(extended[0], start_at, max_tiles, 0)
        inner = jnp.einsum("jrb,rc->jbc", related, result_x, preferred_element_type=jnp.float32)
        keep = (jnp.arange(max_tiles, dtype=jnp.int32) < width_unit[unit_idx]).astype(jnp.float32)
        diag_block = (
            diag_inverse[0, unit_idx].astype(jnp.float32).reshape(max_tiles, block, block) - inner
        ) * keep[:, None, None]
        return (result_x, diag_block.reshape(max_tiles * block, block).astype(jnp.bfloat16))

    off_diag, diag_panels = lax.map(per_unit, jnp.arange(local_units, dtype=jnp.int32))
    return (off_diag[None], diag_panels[None])


def solution(mesh):
    placed = (
        P("grp", "dev"),
        P("grp", "dev", None, None),
        P("grp", "dev", None, None),
        P("grp", None),
        P("grp", None, None),
    )
    return jax.shard_map(
        on_device,
        mesh=mesh,
        in_specs=placed,
        out_specs=(P("grp", "dev", None, None), P("grp", "dev", None, None)),
        check_vma=False,
    )
```

profile of v0, /device:TPU:73, one launch (start us, length us, event | category | flops | bytes accessed | tf_op | source)
XLA Modules:
  0.0 485.8 jit_solution(15844366094010139155)
XLA Ops:
  20.3 56.5 %collective-permute-done = bf16[1,5,2048,128]{2,3,1,0:T(8,128)(2,1)} collective-permute-done((bf16[1,5,2048,128]{2,3,1,0:T(8,128)(2,1)}, bf16[1,5,2048,128]{2,3,1,0:T(8,128)(2,1)}, u32[]{:S(2)}, u32[]{:S(2)}) %collective-permute-start) | collective-permute-done | bytes 2621472 | tf_op jit(solution)/shard_map/ppermute | solution.py:15
  79.8 6.3 %pad_maximum_fusion = bf16[1,16,2048,128]{2,3,1,0:T(8,128)(2,1)} fusion(bf16[1,5,2048,128]{2,3,1,0:T(8,128)(2,1)} %collective-permute-done.1, bf16[1,6,2048,128]{2,3,1,0:T(8,128)(2,1)S(1)} %copy.21, bf16[1,5,2048,128]{2,3,1,0:T(8,128)(2,1)} %collective-permute-done), kind=kLoop, calls=%fused_computation.29 | loop fusion | flops 8388608 | bytes 16777216 | tf_op jit(solution)/shard_map/concatenate | solution.py:13
  86.2 80.3 %all-gather.3.cloned.1.call-done = bf16[65536,256]{1,0:T(8,128)(2,1)} async-done(((bf16[512,256]{1,0:T(8,128)(2,1)}), bf16[65536,256]{1,0:T(8,128)(2,1)}) %all-gather.3.cloned.1.call-update) | async-done | bytes 33554448 | tf_op jit(solution)/shard_map/all_gather | solution.py:29
  166.4 31.2 %copy.25 = bf16[8,16,512,256]{3,1,2,0:T(8,128)(2,1)} copy(bf16[8,16,512,256]{3,2,1,0:T(8,128)(2,1)} %bitcast.82) | data formatting | bytes 67108864 | tf_op jit(solution)/shard_map/reshape | solution.py:30
  197.6 49.9 %reshape_reshape.3 = bf16[32,128,4096]{2,1,0:T(8,128)(2,1)} reshape(bf16[8,512,16,256]{3,2,1,0:T(8,128)(2,1)} %bitcast.81) | data formatting | bytes 67108864 | tf_op jit(solution)/shard_map/reshape;reshape | solution.py:41
  247.5 231.5 %while.17 = (s32[]{:T(128)}, bf16[6,2048,128]{2,1,0:T(8,128)(2,1)}, bf16[6,768,128]{2,1,0:T(8,128)(2,1)}, s32[6]{0:T(128)S(1)}, s32[6,16]{1,0:T(8,128)S(1)}, /*i...) while((s32[]{:T(128)}, bf16[6,2048,128]{2,1,0:T(8,128)(2,1)}, ...), condition=%wide.region_6.7_spmd.clone, body=%wide.region_5.6_spmd.clone.sunk | while | flops 2576746240 | bytes 96605016 | solution.py:74
  256.8 11.8 %gather_fusion = bf16[16,128,4096]{2,1,0:T(8,128)(2,1)} fusion(bf16[32,128,4096]{2,1,0:T(8,128)(2,1)} %get-tuple-element.407, s32[1024]{0:T(1024)S(1)} %pad_clamp_fusion.2), kind=kCustom, calls=%fused_computation.clone.clone.1 | custom fusion | bytes 33554496 | tf_op jit(solution)/shard_map/while/body/eval_jaxpr/jit(_take)/gather | solution.py:58
  268.5 8.5 %broadcast_select_fusion.2 = bf16[16,128,4096]{2,1,0:T(8,128)(2,1)S(1)} fusion(bf16[16,128,4096]{2,1,0:T(8,128)(2,1)} %gather_fusion, pred[16]{0:T(512)(128)(4,1)S(1)} %get-tuple-element.366), kind=kLoop, calls=%fused_computation.3.clone.1 | loop fusion | flops 8388608 | bytes 33554448 | tf_op jit(solution)/shard_map/while/body/eval_jaxpr/jit(_take)/select_n | solution.py:58
  277.1 5.5 %bitcast_dynamic-update-slice_fusion.4 = (bf16[6,2048,128]{2,1,0:T(8,128)(2,1)}, bf16[2048,128]{1,0:T(8,128)(2,1)S(1)}) fusion(bf16[6,2048,128]{2,1,0:T(8,128)(2,1)} %get-tuple-element.387, s32[]{:T(128)S(6)} %copy.31, bf16[2048,4096]{1,0:T(8,128)(2,1)S(1)} %bitcast.80, bf16[4096,128]{1,0:T(8,128)(2,1)S(1)} %reshape.215), kind=kOutput, calls=%fused_computation.13.clone.1 | convolution fusion | flops 2148007936 | bytes 18874372 | tf_op jit(solution)/shard_map/while/body/eval_jaxpr/dot_general | solution.py:63
  295.4 11.8 %gather_fusion = bf16[16,128,4096]{2,1,0:T(8,128)(2,1)} fusion(bf16[32,128,4096]{2,1,0:T(8,128)(2,1)} %get-tuple-element.407, s32[1024]{0:T(1024)S(1)} %pad_clamp_fusion.2), kind=kCustom, calls=%fused_computation.clone.clone.1 | custom fusion | bytes 33554496 | tf_op jit(solution)/shard_map/while/body/eval_jaxpr/jit(_take)/gather | solution.py:58
  307.1 8.5 %broadcast_select_fusion.2 = bf16[16,128,4096]{2,1,0:T(8,128)(2,1)S(1)} fusion(bf16[16,128,4096]{2,1,0:T(8,128)(2,1)} %gather_fusion, pred[16]{0:T(512)(128)(4,1)S(1)} %get-tuple-element.366), kind=kLoop, calls=%fused_computation.3.clone.1 | loop fusion | flops 8388608 | bytes 33554448 | tf_op jit(solution)/shard_map/while/body/eval_jaxpr/jit(_take)/select_n | solution.py:58
  315.6 5.5 %bitcast_dynamic-update-slice_fusion.4 = (bf16[6,2048,128]{2,1,0:T(8,128)(2,1)}, bf16[2048,128]{1,0:T(8,128)(2,1)S(1)}) fusion(bf16[6,2048,128]{2,1,0:T(8,128)(2,1)} %get-tuple-element.387, s32[]{:T(128)S(6)} %copy.31, bf16[2048,4096]{1,0:T(8,128)(2,1)S(1)} %bitcast.80, bf16[4096,128]{1,0:T(8,128)(2,1)S(1)} %reshape.215), kind=kOutput, calls=%fused_computation.13.clone.1 | convolution fusion | flops 2148007936 | bytes 18874372 | tf_op jit(solution)/shard_map/while/body/eval_jaxpr/dot_general | solution.py:63
  333.9 11.8 %gather_fusion = bf16[16,128,4096]{2,1,0:T(8,128)(2,1)} fusion(bf16[32,128,4096]{2,1,0:T(8,128)(2,1)} %get-tuple-element.407, s32[1024]{0:T(1024)S(1)} %pad_clamp_fusion.2), kind=kCustom, calls=%fused_computation.clone.clone.1 | custom fusion | bytes 33554496 | tf_op jit(solution)/shard_map/while/body/eval_jaxpr/jit(_take)/gather | solution.py:58
  345.7 8.5 %broadcast_select_fusion.2 = bf16[16,128,4096]{2,1,0:T(8,128)(2,1)S(1)} fusion(bf16[16,128,4096]{2,1,0:T(8,128)(2,1)} %gather_fusion, pred[16]{0:T(512)(128)(4,1)S(1)} %get-tuple-element.366), kind=kLoop, calls=%fused_computation.3.clone.1 | loop fusion | flops 8388608 | bytes 33554448 | tf_op jit(solution)/shard_map/while/body/eval_jaxpr/jit(_take)/select_n | solution.py:58
  354.2 5.5 %bitcast_dynamic-update-slice_fusion.4 = (bf16[6,2048,128]{2,1,0:T(8,128)(2,1)}, bf16[2048,128]{1,0:T(8,128)(2,1)S(1)}) fusion(bf16[6,2048,128]{2,1,0:T(8,128)(2,1)} %get-tuple-element.387, s32[]{:T(128)S(6)} %copy.31, bf16[2048,4096]{1,0:T(8,128)(2,1)S(1)} %bitcast.80, bf16[4096,128]{1,0:T(8,128)(2,1)S(1)} %reshape.215), kind=kOutput, calls=%fused_computation.13.clone.1 | convolution fusion | flops 2148007936 | bytes 18874372 | tf_op jit(solution)/shard_map/while/body/eval_jaxpr/dot_general | solution.py:63
  372.5 11.8 %gather_fusion = bf16[16,128,4096]{2,1,0:T(8,128)(2,1)} fusion(bf16[32,128,4096]{2,1,0:T(8,128)(2,1)} %get-tuple-element.407, s32[1024]{0:T(1024)S(1)} %pad_clamp_fusion.2), kind=kCustom, calls=%fused_computation.clone.clone.1 | custom fusion | bytes 33554496 | tf_op jit(solution)/shard_map/while/body/eval_jaxpr/jit(_take)/gather | solution.py:58
  384.3 8.5 %broadcast_select_fusion.2 = bf16[16,128,4096]{2,1,0:T(8,128)(2,1)S(1)} fusion(bf16[16,128,4096]{2,1,0:T(8,128)(2,1)} %gather_fusion, pred[16]{0:T(512)(128)(4,1)S(1)} %get-tuple-element.366), kind=kLoop, calls=%fused_computation.3.clone.1 | loop fusion | flops 8388608 | bytes 33554448 | tf_op jit(solution)/shard_map/while/body/eval_jaxpr/jit(_take)/select_n | solution.py:58
  392.8 5.5 %bitcast_dynamic-update-slice_fusion.4 = (bf16[6,2048,128]{2,1,0:T(8,128)(2,1)}, bf16[2048,128]{1,0:T(8,128)(2,1)S(1)}) fusion(bf16[6,2048,128]{2,1,0:T(8,128)(2,1)} %get-tuple-element.387, s32[]{:T(128)S(6)} %copy.31, bf16[2048,4096]{1,0:T(8,128)(2,1)S(1)} %bitcast.80, bf16[4096,128]{1,0:T(8,128)(2,1)S(1)} %reshape.215), kind=kOutput, calls=%fused_computation.13.clone.1 | convolution fusion | flops 2148007936 | bytes 18874372 | tf_op jit(solution)/shard_map/while/body/eval_jaxpr/dot_general | solution.py:63
  411.1 11.8 %gather_fusion = bf16[16,128,4096]{2,1,0:T(8,128)(2,1)} fusion(bf16[32,128,4096]{2,1,0:T(8,128)(2,1)} %get-tuple-element.407, s32[1024]{0:T(1024)S(1)} %pad_clamp_fusion.2), kind=kCustom, calls=%fused_computation.clone.clone.1 | custom fusion | bytes 33554496 | tf_op jit(solution)/shard_map/while/body/eval_jaxpr/jit(_take)/gather | solution.py:58
  422.9 8.5 %broadcast_select_fusion.2 = bf16[16,128,4096]{2,1,0:T(8,128)(2,1)S(1)} fusion(bf16[16,128,4096]{2,1,0:T(8,128)(2,1)} %gather_fusion, pred[16]{0:T(512)(128)(4,1)S(1)} %get-tuple-element.366), kind=kLoop, calls=%fused_computation.3.clone.1 | loop fusion | flops 8388608 | bytes 33554448 | tf_op jit(solution)/shard_map/while/body/eval_jaxpr/jit(_take)/select_n | solution.py:58
  431.4 5.5 %bitcast_dynamic-update-slice_fusion.4 = (bf16[6,2048,128]{2,1,0:T(8,128)(2,1)}, bf16[2048,128]{1,0:T(8,128)(2,1)S(1)}) fusion(bf16[6,2048,128]{2,1,0:T(8,128)(2,1)} %get-tuple-element.387, s32[]{:T(128)S(6)} %copy.31, bf16[2048,4096]{1,0:T(8,128)(2,1)S(1)} %bitcast.80, bf16[4096,128]{1,0:T(8,128)(2,1)S(1)} %reshape.215), kind=kOutput, calls=%fused_computation.13.clone.1 | convolution fusion | flops 2148007936 | bytes 18874372 | tf_op jit(solution)/shard_map/while/body/eval_jaxpr/dot_general | solution.py:63
  449.7 11.8 %gather_fusion = bf16[16,128,4096]{2,1,0:T(8,128)(2,1)} fusion(bf16[32,128,4096]{2,1,0:T(8,128)(2,1)} %get-tuple-element.407, s32[1024]{0:T(1024)S(1)} %pad_clamp_fusion.2), kind=kCustom, calls=%fused_computation.clone.clone.1 | custom fusion | bytes 33554496 | tf_op jit(solution)/shard_map/while/body/eval_jaxpr/jit(_take)/gather | solution.py:58
  461.4 8.5 %broadcast_select_fusion.2 = bf16[16,128,4096]{2,1,0:T(8,128)(2,1)S(1)} fusion(bf16[16,128,4096]{2,1,0:T(8,128)(2,1)} %gather_fusion, pred[16]{0:T(512)(128)(4,1)S(1)} %get-tuple-element.366), kind=kLoop, calls=%fused_computation.3.clone.1 | loop fusion | flops 8388608 | bytes 33554448 | tf_op jit(solution)/shard_map/while/body/eval_jaxpr/jit(_take)/select_n | solution.py:58
  470.0 5.5 %bitcast_dynamic-update-slice_fusion.4 = (bf16[6,2048,128]{2,1,0:T(8,128)(2,1)}, bf16[2048,128]{1,0:T(8,128)(2,1)S(1)}) fusion(bf16[6,2048,128]{2,1,0:T(8,128)(2,1)} %get-tuple-element.387, s32[]{:T(128)S(6)} %copy.31, bf16[2048,4096]{1,0:T(8,128)(2,1)S(1)} %bitcast.80, bf16[4096,128]{1,0:T(8,128)(2,1)S(1)} %reshape.215), kind=kOutput, calls=%fused_computation.13.clone.1 | convolution fusion | flops 2148007936 | bytes 18874372 | tf_op jit(solution)/shard_map/while/body/eval_jaxpr/dot_general | solution.py:63
  (108 shorter events, 72.5 us)
Async XLA Ops:
  7.2 159.3 %all-gather.3.cloned.1.call-start = ((), (), s32[]{:S(2)}) async-start(), calls=%async_computation | async-start | bytes 33816576 | tf_op jit(solution)/shard_map/all_gather | solution.py:29
  11.1 8.3 %copy-start.1 = (s32[1,32]{1,0:T(1,128)S(1)}, s32[1,32]{1,0:T(1,128)}, u32[]{:S(2)}) copy-start(s32[1,32]{1,0:T(1,128)} %param.10) | copy-start | bytes 388
  11.1 8.8 %copy-start = (s32[1,32,16]{1,2,0:T(8,128)S(1)}, s32[1,32,16]{1,2,0:T(8,128)}, u32[]{:S(2)}) copy-start(s32[1,32,16]{1,2,0:T(8,128)} %param.11) | copy-start | bytes 6148
  14.1 62.7 %collective-permute-start = (bf16[1,5,2048,128]{2,3,1,0:T(8,128)(2,1)}, bf16[1,5,2048,128]{2,3,1,0:T(8,128)(2,1)}, u32[]{:S(2)}, u32[]{:S(2)}) collective-permute-start(bf16[1,5,2048,128]{2,3,1,0:T(8,128)(2,1)} %get-tuple-element.293), channel_id=1, source_target_pairs={{0,1},{1,2},{2,3},{3,4},{4,5},{5,6},{6,7},{7,8},{8,9},{9,10},{10,1... | collective-permute-start | bytes 7864328 | tf_op jit(solution)/shard_map/ppermute | solution.py:15
  17.4 62.5 %collective-permute-start.1 = (bf16[1,5,2048,128]{2,3,1,0:T(8,128)(2,1)}, bf16[1,5,2048,128]{2,3,1,0:T(8,128)(2,1)}, u32[]{:S(2)}, u32[]{:S(2)}) collective-permute-start(bf16[1,5,2048,128]{2,3,1,0:T(8,128)(2,1)} %get-tuple-element.294), channel_id=1, source_target_pairs={{1,0},{2,1},{3,2},{4,3},{5,4},{6,5},{7,6},{8,7},{9,8},{10,9},{11,1... | collective-permute-start | bytes 7864328 | tf_op jit(solution)/shard_map/ppermute | solution.py:17
Sparse Core Ops, SparseCore 0:
  11.1 155.2 all-gather.2
where the time goes:
time: 492 us; the launch traced here: 486 us
  local copies, waits for them, and re-layouts  190 us (39%)
  waiting for transfers between devices  140 us (28%)
  other arithmetic  62.4 us (13%)
  matrix products  52.4 us (11%)
  loops' own time  20.7 us (4%)
  between operations  14.1 us (3%)
  starting transfers between devices  5.31 us (1%)
    all_gather x1, waiting for transfers between devices, on_device(): stacked = lax.all_gather(sep_inv[None], ('grp', 'dev'), axis=0, tiled=True)  80.3 us
    gather x6, local copies, waits for them, and re-layouts, per_unit(): rows_pick = jnp.take(row_tiles, chosen, axis=0).reshape(anc_rows, sep_order)  70.6 us
    ppermute x1, waiting for transfers between devices, extended_2(): lax.ppermute(tail, axis, [(i, (i + 1) % count) for i in range(ends)])  56.5 us
    select_n x12, other arithmetic, per_unit(): rows_pick = jnp.take(row_tiles, chosen, axis=0).reshape(anc_rows, sep_order)  51.1 us
    another operation x1, local copies, waits for them, and re-layouts, on_device(): row_tiles = whole_sep.reshape(count_blocks, block, sep_order)  49.9 us
    dot_general x6, matrix products, per_unit(): product = jnp.dot(rows_pick, spread, preferred_element_type=jnp.float32)  32.8 us
    reshape x1, local copies, waits for them, and re-layouts, on_device(): stacked.reshape(group_count, device_count, rows_local, cols_local)  31.2 us
    another operation x1, loops' own time, on_device(): lax.map(per_unit, jnp.arange(local_units, dtype=jnp.int32))  20.7 us
  transfers between devices with their start and end apart: 3, of which 3 were waited for; matrix products, arithmetic and copies ran while one was open for 3% of the time, Pallas kernels for 0%

commit v1 on v0

v1 whole, which is shorter than its diff:
```python
import functools

import jax
import jax.numpy as jnp
from jax import lax
from jax.experimental import pallas as pl
from jax.experimental.pallas import tpu as pltpu
from jax.sharding import Mesh, PartitionSpec as P

T = 128
ALL = ("x", "core", "y", "z")


def compute(meta, row_at, col_at, parts, panels, turned, dinv):
    units, rows, _ = panels.shape
    anc = rows // T
    wmax = dinv.shape[1] // T
    side = wmax - 1
    per_part = [p.shape[0] for p in parts]
    n_parts = len(parts)
    tiles = sum(per_part)
    group = 4

    def kernel(*refs):
        meta_ref, row_ref, col_ref = refs[:3]
        part_refs = refs[3 : 3 + n_parts]
        pan_ref, left_ref, own_ref, right_ref, dinv_ref, off_ref, diag_ref = refs[3 + n_parts : 10 + n_parts]
        sep_v, turn_v, rhs_v, res_v, sem, tsem = refs[10 + n_parts :]
        base = 0
        copies = []
        for i, p in enumerate(part_refs):
            copies.append(pltpu.make_async_copy(p, sep_v.at[pl.ds(base, per_part[i])], sem.at[i]))
            base += per_part[i]
        for c in copies:
            c.start()
        turns = [
            pltpu.make_async_copy(left_ref, turn_v.at[pl.ds(0, side)], tsem.at[0]),
            pltpu.make_async_copy(own_ref, turn_v.at[pl.ds(side, units)], tsem.at[1]),
            pltpu.make_async_copy(right_ref, turn_v.at[pl.ds(side + units, side)], tsem.at[2]),
        ]
        for c in turns:
            c.start()
        for c in copies + turns:
            c.wait()

        def job(t, carry):
            @pl.when(meta_ref[t, 0] == 1)
            def _():
                mate = meta_ref[t, 1]
                first = meta_ref[t, 2]
                width = meta_ref[t, 3]
                rhs_v[:, :T] = pan_ref[t]
                rhs_v[:, T:] = pan_ref[mate]

                def rows_of(a0, carry):
                    lhs = []
                    for i in range(group):
                        r = meta_ref[t, 4 + a0 * group + i]
                        kind = row_ref[1, r]
                        at = row_ref[0, r]
                        lhs.append(
                            jnp.concatenate(
                                [sep_v[at + col_ref[kind, meta_ref[t, 4 + b]]] for b in range(anc)], axis=1
                            )
                        )
                    lhs = jnp.concatenate(lhs, axis=0)
                    prod = jnp.dot(lhs, rhs_v[...], preferred_element_type=jnp.float32)
                    got = (-prod).astype(jnp.bfloat16)
                    here = pl.ds(pl.multiple_of(a0 * group * T, T), group * T)
                    res_v[here, :] = got
                    off_ref[t, here, :] = got[:, :T]
                    off_ref[mate, here, :] = got[:, T:]
                    return carry

                lax.fori_loop(0, anc // group, rows_of, 0)
                for j in range(wmax):
                    inner = jnp.dot(turn_v[first + j], res_v[...], preferred_element_type=jnp.float32)
                    live = j < width
                    here = slice(j * T, (j + 1) * T)
                    for k, u in ((1, mate), (0, t)):
                        new = dinv_ref[u, here, :].astype(jnp.float32) - inner[:, k * T : (k + 1) * T]
                        diag_ref[u, here, :] = jnp.where(live, new, 0.0).astype(jnp.bfloat16)

            return carry

        lax.fori_loop(0, units, job, 0)

    any_spec = pl.BlockSpec(memory_space=pl.ANY)
    vmem_spec = pl.BlockSpec(memory_space=pltpu.VMEM)
    smem_spec = pl.BlockSpec(memory_space=pltpu.SMEM)
    return pl.pallas_call(
        kernel,
        out_shape=(
            jax.ShapeDtypeStruct(panels.shape, jnp.bfloat16),
            jax.ShapeDtypeStruct(dinv.shape, jnp.bfloat16),
        ),
        in_specs=[smem_spec] * 3 + [any_spec] * n_parts + [vmem_spec] + [any_spec] * 3 + [vmem_spec],
        out_specs=(vmem_spec, vmem_spec),
        scratch_shapes=[
            pltpu.VMEM((tiles, T, T), jnp.bfloat16),
            pltpu.VMEM((units + 2 * side, T, rows), jnp.bfloat16),
            pltpu.VMEM((rows, 2 * T), jnp.bfloat16),
            pltpu.VMEM((rows, 2 * T), jnp.bfloat16),
            pltpu.SemaphoreType.DMA((n_parts,)),
            pltpu.SemaphoreType.DMA((3,)),
        ],
        compiler_params=pltpu.CompilerParams(vmem_limit_bytes=64 * 1024 * 1024),
        cost_estimate=pl.CostEstimate(flops=2 * 7 * rows * rows * T * units // 6, bytes_accessed=50_000_000, transcendentals=0),
        name="units",
    )(meta, row_at, col_at, *parts, panels, *turned, dinv)


def unit_table(widths, ancestors, place, units):
    wmax = 6
    ends = jnp.cumsum(widths)
    starts = ends - widths
    local = jnp.arange(units, dtype=jnp.int32)
    position = place * units + local
    owner = jnp.sum((ends[None, :] <= position[:, None]).astype(jnp.int32), axis=1)
    hot = (jnp.arange(widths.shape[0], dtype=jnp.int32)[None, :] == owner[:, None]).astype(jnp.int32)
    column = position - jnp.sum(hot * starts[None, :], axis=1)
    width = jnp.sum(hot * widths[None, :], axis=1)
    blocks = jnp.sum(hot[:, :, None] * ancestors[None, :, :], axis=1)
    run = jnp.minimum(column, local)
    leads = (run % 2 == 0).astype(jnp.int32)
    mate = jnp.where((column + 1 < width) & (local + 1 < units), local + 1, local)
    first = (wmax - 1) + local - column
    return jnp.concatenate([jnp.stack([leads, mate, first, width], axis=1), blocks], axis=1).astype(jnp.int32)


def on_device(sep, panels, dinv, widths, ancestors):
    panels, dinv, widths, ancestors = panels[0], dinv[0], widths[0], ancestors[0]
    units = panels.shape[0]
    side = dinv.shape[1] // T - 1
    n_y, n_z = lax.axis_size("y"), lax.axis_size("z")
    n_dev = n_y * n_z
    rt, ct = sep.shape[0] // T, sep.shape[1] // T
    shard = sep.reshape(rt, T, ct, T).transpose(0, 2, 1, 3)
    whole = lax.all_gather(shard[None], ALL, axis=0, tiled=True)
    n_tiles = whole.shape[0] * rt * ct
    whole = whole.reshape(n_tiles, T, T)
    steps = [(i, i + 1) for i in range(n_dev - 1)]
    left = lax.ppermute(panels[units - side :], ("y", "z"), steps)
    right = lax.ppermute(panels[:side], ("y", "z"), [(b, a) for a, b in steps])
    turned = [v.transpose(0, 2, 1) for v in (left, panels, right)]
    place = lax.axis_index("y") * n_z + lax.axis_index("z")
    meta = unit_table(widths, ancestors, place, units)
    count = lax.axis_size("x") * lax.axis_size("core") * rt
    tile = jnp.arange(count, dtype=jnp.int32)
    row_at = jnp.stack([(tile // rt) * (n_dev * rt * ct) + (tile % rt) * ct, jnp.zeros_like(tile)])
    col_at = ((tile // ct) * (rt * ct) + tile % ct)[None]
    off, diag = compute(meta, row_at, col_at, [whole], panels, turned, dinv)
    return off[None], diag[None]


def solution(mesh):
    grid = Mesh(mesh.devices.reshape(4, 2, 4, 4), ALL)
    grp, dev = ("x", "core"), ("y", "z")
    placed = (P(grp, dev), P(grp, dev), P(grp, dev), P(grp), P(grp))
    return jax.shard_map(
        on_device, mesh=grid, in_specs=placed, out_specs=(P(grp, dev), P(grp, dev)), check_vma=False
    )
```

time: 492 us -> 213 us (0.43)
  local copies, waits for them, and re-layouts: 190 us -> 9.88 us
  other arithmetic: 62.4 us -> 1.42 us
  matrix products: 52.4 us -> 0 us
  Pallas kernels: 0 us -> 33.7 us
  loops' own time: 20.7 us -> 0 us
    gather x6 -> x0, local copies, waits for them, and re-layouts: 70.6 us -> none  [per_unit(): rows_pick = jnp.take(row_tiles, chosen, axis=0).reshape(anc_rows, sep_order)]
    dot_general x18 -> x0, matrix products: 52.4 us -> none  [the longest x6 32.8 us: per_unit(): product = jnp.dot(rows_pick, spread, preferred_element_type=jnp.float32)]
    select_n x12 -> x0, other arithmetic: 51.1 us -> none  [per_unit(): rows_pick = jnp.take(row_tiles, chosen, axis=0).reshape(anc_rows, sep_order)]
    another operation x1, local copies, waits for them, and re-layouts: 49.9 us -> 0.59 us  [on_device(): jnp.stack([tile // rt * (n_dev * rt * ct) + tile % rt * ct, jnp.zeros_lik...]
    pallas_call x0 -> x1, Pallas kernels: none -> 33.7 us  [compute(): pl.pallas_call(kernel, out_shape=(jax.ShapeDtypeStruct(panels.shape, jnp....]
    reshape x8 -> x2, local copies, waits for them, and re-layouts: 34.4 us -> 1.1 us  [the longest x1 1.02 us: on_device(): shard = sep.reshape(rt, T, ct, T).transpose(0, 2, 1, 3)]
    dynamic_slice x30 -> x0, local copies, waits for them, and re-layouts: 23.9 us -> none  [the longest x6 6.49 us: per_unit(): panel_flat = panels[0, unit_idx].reshape(anc_tiles, block * block)]
    another operation x1 -> x0, loops' own time: 20.7 us -> none  [on_device(): lax.map(per_unit, jnp.arange(local_units, dtype=jnp.int32))]
  transfers between devices with their start and end apart: 3 -> 3, of which waited for: 3 -> 3; matrix products, arithmetic and copies ran while one was open for 3% -> 5% of each run, Pallas kernels for 0% -> 0%
where the time goes in v1:
time: 213 us; the launch traced here: 209 us
  waiting for transfers between devices  144 us (68%)
  Pallas kernels  33.7 us (16%)
  between operations  14.1 us (7%)
  local copies, waits for them, and re-layouts  9.88 us (5%)
  starting transfers between devices  5.31 us (2%)
    all_gather x1, waiting for transfers between devices, on_device(): whole = lax.all_gather(shard[None], ALL, axis=0, tiled=True)  87.9 us
    ppermute x1, waiting for transfers between devices, on_device(): right = lax.ppermute(panels[:side], ('y', 'z'), [(b, a) for a, b in steps])  54.5 us
    pallas_call x1, Pallas kernels, compute(): pl.pallas_call(kernel, out_shape=(jax.ShapeDtypeStruct(panels.shape, jnp....  33.7 us
  transfers between devices with their start and end apart: 3, of which 3 were waited for; matrix products, arithmetic and copies ran while one was open for 5% of the time, Pallas kernels for 0%

profile of v1, /device:TPU:73, one launch (start us, length us, event | category | flops | bytes accessed | tf_op | source)
XLA Modules:
  0.0 208.7 jit_solution(1428574072350797679)
XLA Ops:
  7.2 0.0 all-gather.3.cloned.1.call-start
  7.2 1.0 reshape.257
  8.2 0.7 copy.50
  9.0 0.0 all-gather.3.cloned.1.call-update
  9.0 3.2 %copy.51 = bf16[1,6,2048,128]{2,3,1,0:T(8,128)(2,1)S(1)} copy(bf16[1,6,2048,128]{3,2,1,0:T(8,128)(2,1)} %param.6) | data formatting | bytes 6291456 | tf_op args[1]
  12.2 3.4 %slice_bitcast_fusion = (bf16[5,2048,128]{1,2,0:T(8,128)(2,1)}, bf16[5,2048,128]{1,2,0:T(8,128)(2,1)}) fusion(bf16[1,6,2048,128]{2,3,1,0:T(8,128)(2,1)S(1)} %copy.51), kind=kLoop, calls=%fused_computation | loop fusion | bytes 10485760 | tf_op jit(solution)/shard_map/slice | solution.py:144
  15.6 1.9 collective-permute-start.1
  17.5 3.4 %collective-permute-start = (bf16[5,2048,128]{1,2,0:T(8,128)(2,1)}, bf16[5,2048,128]{1,2,0:T(8,128)(2,1)}, u32[]{:S(2)}, u32[]{:S(2)}) collective-permute-start(bf16[5,2048,128]{1,2,0:T(8,128)(2,1)} %get-tuple-element.9), channel_id=1, source_target_pairs={{0,1},{1,2},{2,3},{3,4},{4,5},{5,6},{6,7},{7,8},{8,9},{9,10},{10,1... | collective-permute-start | bytes 7864328 | tf_op jit(solution)/shard_map/ppermute | solution.py:143
  20.9 0.1 copy.46
  21.0 0.6 stack.2.refs_1_
  21.6 0.1 reduce-window.4
  21.7 0.1 reduce
  21.8 0.2 convert_reduce_fusion
  22.0 0.2 select_reduce_fusion
  22.2 0.1 copy.47
  22.3 0.1 copy.48
  22.4 0.1 fusion.3
  22.4 0.2 multiply_reduce_fusion
  22.6 0.7 concatenate.3.refs_0_
  23.3 0.6 fusion.6.refs_2_
  23.9 54.5 %collective-permute-done.1 = bf16[5,2048,128]{1,2,0:T(8,128)(2,1)} collective-permute-done((bf16[5,2048,128]{1,2,0:T(8,128)(2,1)}, bf16[5,2048,128]{1,2,0:T(8,128)(2,1)}, u32[]{:S(2)}, u32[]{:S(2)}) %collective-permute-start.1) | collective-permute-done | bytes 2621472 | tf_op jit(solution)/shard_map/ppermute | solution.py:144
  78.4 1.8 collective-permute-done
  80.2 87.9 %all-gather.3.cloned.1.call-done = bf16[512,2,128,128]{3,2,1,0:T(8,128)(2,1)} async-done(((bf16[4,2,128,128]{3,2,1,0:T(8,128)(2,1)}), bf16[512,2,128,128]{3,2,1,0:T(8,128)(2,1)}) %all-gather.3.cloned.1.call-update) | async-done | bytes 33554448 | tf_op jit(solution)/shard_map/all_gather | solution.py:139
  168.1 33.7 %units.1 = (bf16[6,2048,128]{2,1,0:T(8,128)(2,1)}, bf16[6,768,128]{2,1,0:T(8,128)(2,1)}) custom-call(s32[6,20]{1,0:T(8,128)} %concatenate.3.refs_0_, s32[2,32]{1,0:T(2,128)} %stack.2.refs_1_, s32[1,32]{1,0:T(1,128)} %fusion.6.refs_2_, bf16[1024,128,128]{2,1,0:T(8,128)(2,1)} %bitcast.27, bf16[6,2048,128]{2,1,0:T(8,128)(2,1)} %bitcast.28, ...), custom_call_target="tpu_custom_call" | custom-call | flops 7516192768 | bytes 50000000 | tf_op jit(solution)/shard_map/units/pallas_call | solution.py:91
  (11 shorter events, 0.1 us)
Async XLA Ops:
  7.2 161.0 %all-gather.3.cloned.1.call-start = ((), (), s32[]{:S(2)}) async-start(), calls=%async_computation | async-start | bytes 33816576 | tf_op jit(solution)/shard_map/all_gather | solution.py:139
  12.2 3.4 %copy-start = (bf16[1,6,2048,128]{2,3,1,0:T(8,128)(2,1)}, bf16[1,6,2048,128]{2,3,1,0:T(8,128)(2,1)S(1)}, u32[]{:S(2)}) copy-start(bf16[1,6,2048,128]{2,3,1,0:T(8,128)(2,1)S(1)} %copy.51) | copy-start | bytes 9437188
  12.2 8.7 %copy-start.2 = (s32[1,32]{1,0:T(1,128)S(1)}, s32[1,32]{1,0:T(1,128)}, u32[]{:S(2)}) copy-start(s32[1,32]{1,0:T(1,128)} %param.8) | copy-start | bytes 388
  12.2 10.2 %copy-start.1 = (s32[1,32,16]{1,2,0:T(8,128)S(1)}, s32[1,32,16]{1,2,0:T(8,128)}, u32[]{:S(2)}) copy-start(s32[1,32,16]{1,2,0:T(8,128)} %param.9) | copy-start | bytes 6148
  15.6 62.7 %collective-permute-start.1 = (bf16[5,2048,128]{1,2,0:T(8,128)(2,1)}, bf16[5,2048,128]{1,2,0:T(8,128)(2,1)}, u32[]{:S(2)}, u32[]{:S(2)}) collective-permute-start(bf16[5,2048,128]{1,2,0:T(8,128)(2,1)} %get-tuple-element.8), channel_id=1, source_target_pairs={{1,0},{2,1},{3,2},{4,3},{5,4},{6,5},{7,6},{8,7},{9,8},{10,9},{11,1... | collective-permute-start | bytes 7864328 | tf_op jit(solution)/shard_map/ppermute | solution.py:144
  17.5 62.7 %collective-permute-start = (bf16[5,2048,128]{1,2,0:T(8,128)(2,1)}, bf16[5,2048,128]{1,2,0:T(8,128)(2,1)}, u32[]{:S(2)}, u32[]{:S(2)}) collective-permute-start(bf16[5,2048,128]{1,2,0:T(8,128)(2,1)} %get-tuple-element.9), channel_id=1, source_target_pairs={{0,1},{1,2},{2,3},{3,4},{4,5},{5,6},{6,7},{7,8},{8,9},{9,10},{10,1... | collective-permute-start | bytes 7864328 | tf_op jit(solution)/shard_map/ppermute | solution.py:143
Sparse Core Ops, SparseCore 0:
  11.7 156.3 all-gather.2

commit v2 on v1

--- a/solution.py
+++ b/solution.py
@@ -1,11 +1,13 @@
-import functools
+import math
 
 import jax
 import jax.numpy as jnp
+import numpy as np
 from jax import lax
 from jax.experimental import pallas as pl
 from jax.experimental.pallas import tpu as pltpu
 from jax.sharding import Mesh, PartitionSpec as P
+
 
 T = 128
 ALL = ("x", "core", "y", "z")
@@ -128,6 +130,69 @@
     return jnp.concatenate([jnp.stack([leads, mate, first, width], axis=1), blocks], axis=1).astype(jnp.int32)
 
 
+ROUTES = ((("z", "y", "x"), ("y", "z", "x")), (("x", "z", "y"), ("z", "x", "y")))
+AXIS = {"x": 0, "y": 2, "z": 3}
+
+
+def neighbours(sizes, dims, by):
+    out = []
+    total = math.prod(sizes)
+    for i in range(total):
+        at = list(np.unravel_index(i, sizes))
+        k = AXIS[dims[at[1]]]
+        at[k] = (at[k] + by) % sizes[k]
+        out.append((i, int(np.ravel_multi_index(at, sizes))))
+    return out
+
+
+def gathered(shard):
+    sizes = [lax.axis_size(a) for a in ALL]
+    halves = len(ROUTES[0])
+    rt = shard.shape[0]
+
+    def send(v, dims, by):
+        return lax.ppermute(v, ALL, neighbours(sizes, dims, by))
+
+    def swap(v):
+        return lax.ppermute(v, "core", [(0, 1), (1, 0)])
+
+    parts = []
+    for h in range(halves):
+        block = shard[h * rt // halves : (h + 1) * rt // halves][None]
+        legs = [tuple(ROUTES[c][h][leg] for c in range(2)) for leg in range(3)]
+        for dims in legs[:2]:
+            up, down, across = (send(block, dims, by) for by in (1, -1, 2))
+            block = jnp.concatenate([block, down, across, up], axis=0)
+        up, down = (send(block, legs[2], by) for by in (1, -1))
+        across = send(up if h == 0 else down, legs[2], 1 if h == 0 else -1)
+        parts += [block, down, across, up]
+    parts += [swap(v) for v in parts]
+    return [v.reshape(-1, T, T) for v in parts]
+
+
+def tile_tables(rt, ct):
+    sizes = {a: lax.axis_size(a) for a in ALL}
+    ring, halves = sizes["x"], len(ROUTES[0])
+    inner = rt // halves * ct
+    r = jnp.arange(ring * 2 * rt, dtype=jnp.int32)
+    c = jnp.arange(sizes["y"] * sizes["z"] * ct, dtype=jnp.int32)
+    ahead = lambda axis, v: (v - lax.axis_index(axis) + ring) % ring
+    off_x = ahead("x", r // (2 * rt))
+    off = {"y": ahead("y", c // (sizes["z"] * ct)), "z": ahead("z", c // ct % sizes["z"])}
+    core, half = r // rt % 2, r % rt // (rt // halves)
+    kind = core * halves + half
+    weight = {a: [] for a in "xyz"}
+    for route in (ROUTES[k // halves][k % halves] for k in range(2 * halves)):
+        for leg, axis in enumerate(route):
+            weight[axis].append(inner * ring**leg)
+    part = inner * ring**3
+    row = jnp.where(core == lax.axis_index("core"), 0, halves * part) + half * part + r % (rt // halves) * ct
+    for k in range(2 * halves):
+        row = row + jnp.where(kind == k, weight["x"][k], 0) * off_x
+    col = jnp.stack([weight["y"][k] * off["y"] + weight["z"][k] * off["z"] + c % ct for k in range(2 * halves)])
+    return jnp.stack([row, kind]), col
+
+
 def on_device(sep, panels, dinv, widths, ancestors):
     panels, dinv, widths, ancestors = panels[0], dinv[0], widths[0], ancestors[0]
     units = panels.shape[0]
@@ -136,20 +201,15 @@
     n_dev = n_y * n_z
     rt, ct = sep.shape[0] // T, sep.shape[1] // T
     shard = sep.reshape(rt, T, ct, T).transpose(0, 2, 1, 3)
-    whole = lax.all_gather(shard[None], ALL, axis=0, tiled=True)
-    n_tiles = whole.shape[0] * rt * ct
-    whole = whole.reshape(n_tiles, T, T)
+    parts = gathered(shard)
     steps = [(i, i + 1) for i in range(n_dev - 1)]
     left = lax.ppermute(panels[units - side :], ("y", "z"), steps)
     right = lax.ppermute(panels[:side], ("y", "z"), [(b, a) for a, b in steps])
     turned = [v.transpose(0, 2, 1) for v in (left, panels, right)]
     place = lax.axis_index("y") * n_z + lax.axis_index("z")
     meta = unit_table(widths, ancestors, place, units)
-    count = lax.axis_size("x") * lax.axis_size("core") * rt
-    tile = jnp.arange(count, dtype=jnp.int32)
-    row_at = jnp.stack([(tile // rt) * (n_dev * rt * ct) + (tile % rt) * ct, jnp.zeros_like(tile)])
-    col_at = ((tile // ct) * (rt * ct) + tile % ct)[None]
-    off, diag = compute(meta, row_at, col_at, [whole], panels, turned, dinv)
+    row_at, col_at = tile_tables(rt, ct)
+    off, diag = compute(meta, row_at, col_at, parts, panels, turned, dinv)
     return off[None], diag[None]
 
 
@@ -157,6 +217,5 @@
     grid = Mesh(mesh.devices.reshape(4, 2, 4, 4), ALL)
     grp, dev = ("x", "core"), ("y", "z")
     placed = (P(grp, dev), P(grp, dev), P(grp, dev), P(grp), P(grp))
-    return jax.shard_map(
-        on_device, mesh=grid, in_specs=placed, out_specs=(P(grp, dev), P(grp, dev)), check_vma=False
-    )
+
+    return jax.shard_map(on_device, mesh=grid, in_specs=placed, out_specs=(P(grp, dev), P(grp, dev)), check_vma=False)

time: 213 us -> 280 us (1.31)
  the two profiles are of different devices: /device:TPU:73 before, /device:TPU:23 now
where the time goes in v2:
time: 280 us
  starting transfers between devices  164 us (59%)
  waiting for transfers between devices  70.2 us (25%)
  Pallas kernels  33.8 us (12%)
  local copies, waits for them, and re-layouts  8.26 us (3%)
    ppermute x8, starting transfers between devices, swap(): return lax.ppermute(v, 'core', [(0, 1), (1, 0)])  93.5 us
    ppermute x18, starting transfers between devices, send(): return lax.ppermute(v, ALL, neighbours(sizes, dims, by))  62.7 us
    ppermute x1, waiting for transfers between devices, on_device(): left = lax.ppermute(panels[units - side:], ('y', 'z'), steps)  45.7 us
    pallas_call x1, Pallas kernels, compute(): pl.pallas_call(kernel, out_shape=(jax.ShapeDtypeStruct(panels.shape, jnp....  33.8 us
    ppermute x18, waiting for transfers between devices, send(): return lax.ppermute(v, ALL, neighbours(sizes, dims, by))  23.3 us
  transfers between devices with their start and end apart: 28, of which 10 were waited for; matrix products, arithmetic and copies ran while one was open for 1% of the time, Pallas kernels for 0%

profile of v2, /device:TPU:23, one launch (start us, length us, event | category | flops | bytes accessed | tf_op | source)
XLA Modules:
  0.0 279.6 jit_solution(2755021806038985143)
XLA Ops:
  0.6 3.2 %copy.32 = bf16[1,6,2048,128]{2,3,1,0:T(8,128)(2,1)S(1)} copy(bf16[1,6,2048,128]{3,2,1,0:T(8,128)(2,1)} %param.6) | data formatting | bytes 6291456 | tf_op args[1]
  3.9 3.4 %slice_bitcast_fusion = (bf16[5,2048,128]{1,2,0:T(8,128)(2,1)}, bf16[5,2048,128]{1,2,0:T(8,128)(2,1)}) fusion(bf16[1,6,2048,128]{2,3,1,0:T(8,128)(2,1)S(1)} %copy.32), kind=kLoop, calls=%fused_computation | loop fusion | bytes 10485760 | tf_op jit(solution)/shard_map/slice | solution.py:207
  7.2 5.5 %collective-permute-start.27 = (bf16[5,2048,128]{1,2,0:T(8,128)(2,1)}, bf16[5,2048,128]{1,2,0:T(8,128)(2,1)S(1)}, u32[]{:S(2)}, u32[]{:S(2)}) collective-permute-start(bf16[5,2048,128]{1,2,0:T(8,128)(2,1)} %get-tuple-element.8), channel_id=1, source_target_pairs={{1,0},{2,1},{3,2},{4,3},{5,4},{6,5},{7,6},{8,7},{9,8},{10,9},{11,1... | collective-permute-start | bytes 7864328 | tf_op jit(solution)/shard_map/ppermute | solution.py:207
  13.2 2.1 collective-permute-start.1
  15.3 1.4 collective-permute-start.10
  18.5 1.6 collective-permute-start
  20.1 3.4 %collective-permute-done = bf16[1,2,2,128,128]{4,3,2,1,0:T(8,128)(2,1)S(1)} collective-permute-done((bf16[1,2,2,128,128]{4,3,2,1,0:T(8,128)(2,1)S(1)}, bf16[1,2,2,128,128]{4,3,2,1,0:T(8,128)(2,1)S(1)}, u32[]{:S(2)}, u32[]{:S(2)}) %collective-permute-start) | collective-permute-done | bytes 131104 | tf_op jit(solution)/shard_map/ppermute | solution.py:154
  23.9 1.9 collective-permute-start.4
  25.7 48.2 %collective-permute-start.3 = (bf16[4,2,2,128,128]{4,3,2,1,0:T(8,128)(2,1)S(1)}, bf16[4,2,2,128,128]{4,3,2,1,0:T(8,128)(2,1)S(1)}, u32[]{:S(2)}, u32[]{:S(2)}) collective-permute-start(bf16[4,2,2,128,128]{4,3,2,1,0:T(8,128)(2,1)S(1)} %pad_maximum_fusion), channel_id=1, source_target_pairs={{0,12},{1,13},{2,14},{3,15},{4,0},{5,1},{6,2},{7,3},{8,4},{9,5},{1... | collective-permute-start | bytes 1572872 | tf_op jit(solution)/shard_map/ppermute | solution.py:154
  73.9 7.0 %collective-permute-done.9 = bf16[1,2,2,128,128]{4,3,2,1,0:T(8,128)(2,1)S(1)} collective-permute-done((bf16[1,2,2,128,128]{4,3,2,1,0:T(8,128)(2,1)S(1)}, bf16[1,2,2,128,128]{4,3,2,1,0:T(8,128)(2,1)S(1)}, u32[]{:S(2)}, u32[]{:S(2)}) %collective-permute-start.9) | collective-permute-done | bytes 131104 | tf_op jit(solution)/shard_map/ppermute | solution.py:154
  82.7 4.8 %collective-permute-done.3 = bf16[4,2,2,128,128]{4,3,2,1,0:T(8,128)(2,1)S(1)} collective-permute-done((bf16[4,2,2,128,128]{4,3,2,1,0:T(8,128)(2,1)S(1)}, bf16[4,2,2,128,128]{4,3,2,1,0:T(8,128)(2,1)S(1)}, u32[]{:S(2)}, u32[]{:S(2)}) %collective-permute-start.3) | collective-permute-done | bytes 524320 | tf_op jit(solution)/shard_map/ppermute | solution.py:154
  87.8 2.4 collective-permute-start.26
  90.5 5.6 %collective-permute-done.12 = bf16[4,2,2,128,128]{4,3,2,1,0:T(8,128)(2,1)S(1)} collective-permute-done((bf16[4,2,2,128,128]{4,3,2,1,0:T(8,128)(2,1)S(1)}, bf16[4,2,2,128,128]{4,3,2,1,0:T(8,128)(2,1)S(1)}, u32[]{:S(2)}, u32[]{:S(2)}) %collective-permute-start.12) | collective-permute-done | bytes 524320 | tf_op jit(solution)/shard_map/ppermute | solution.py:154
  96.1 7.9 %collective-permute-start.18 = (bf16[16,2,2,128,128]{4,3,2,1,0:T(8,128)(2,1)S(1)}, bf16[16,2,2,128,128]{4,3,2,1,0:T(8,128)(2,1)S(1)}, u32[]{:S(2)}, u32[]{:S(2)}) collective-permute-start(bf16[16,2,2,128,128]{4,3,2,1,0:T(8,128)(2,1)S(1)} %constant_dynamic-update-slice_fusion), channel_id=1, source_target_pairs={{0,16},{16,0},{1,17},{17,1},{2,18},{18,2},{3,19},{19,3},{4,20},{20... | collective-permute-start | bytes 6291464 | tf_op jit(solution)/shard_map/ppermute | solution.py:157
  104.1 1.4 collective-permute-start.7
  107.1 45.7 %collective-permute-done.26 = bf16[5,2048,128]{1,2,0:T(8,128)(2,1)S(1)} collective-permute-done((bf16[5,2048,128]{1,2,0:T(8,128)(2,1)S(1)}, bf16[5,2048,128]{1,2,0:T(8,128)(2,1)S(1)}, u32[]{:S(2)}, u32[]{:S(2)}) %collective-permute-start.26) | collective-permute-done | bytes 2621472 | tf_op jit(solution)/shard_map/ppermute | solution.py:206
  152.8 15.9 %collective-permute-start.22 = (bf16[16,2,2,128,128]{4,3,2,1,0:T(8,128)(2,1)S(1)}, bf16[16,2,2,128,128]{4,3,2,1,0:T(8,128)(2,1)S(1)}, u32[]{:S(2)}, u32[]{:S(2)}) collective-permute-start(bf16[16,2,2,128,128]{4,3,2,1,0:T(8,128)(2,1)S(1)} %constant_dynamic-update-slice_fusion.7), channel_id=1, source_target_pairs={{0,16},{16,0},{1,17},{17,1},{2,18},{18,2},{3,19},{19,3},{4,20},{20... | collective-permute-start | bytes 6291464 | tf_op jit(solution)/shard_map/ppermute | solution.py:157
  168.8 2.0 collective-permute-start.21
  170.9 1.5 collective-permute-start.16
  172.5 41.9 %collective-permute-start.23 = (bf16[16,2,2,128,128]{4,3,2,1,0:T(8,128)(2,1)}, bf16[16,2,2,128,128]{4,3,2,1,0:T(8,128)(2,1)}, u32[]{:S(2)}, u32[]{:S(2)}) collective-permute-start(bf16[16,2,2,128,128]{4,3,2,1,0:T(8,128)(2,1)} %collective-permute-done.15), channel_id=1, source_target_pairs={{0,16},{16,0},{1,17},{17,1},{2,18},{18,2},{3,19},{19,3},{4,20},{20... | collective-permute-start | bytes 6291464 | tf_op jit(solution)/shard_map/ppermute | solution.py:157
  215.1 1.5 collective-permute-done.8
  216.5 2.3 collective-permute-start.20
  218.9 22.8 %collective-permute-start.24 = (bf16[16,2,2,128,128]{4,3,2,1,0:T(8,128)(2,1)}, bf16[16,2,2,128,128]{4,3,2,1,0:T(8,128)(2,1)}, u32[]{:S(2)}, u32[]{:S(2)}) collective-permute-start(bf16[16,2,2,128,128]{4,3,2,1,0:T(8,128)(2,1)} %collective-permute-done.16), channel_id=1, source_target_pairs={{0,16},{16,0},{1,17},{17,1},{2,18},{18,2},{3,19},{19,3},{4,20},{20... | collective-permute-start | bytes 6291464 | tf_op jit(solution)/shard_map/ppermute | solution.py:157
  245.8 33.8 %units.1 = (bf16[6,2048,128]{2,1,0:T(8,128)(2,1)}, bf16[6,768,128]{2,1,0:T(8,128)(2,1)}) custom-call(s32[6,20]{1,0:T(8,128)} %concatenate.17.refs_0_, s32[2,32]{1,0:T(2,128)} %pad_add_fusion.1.refs_1_, s32[4,32]{1,0:T(4,128)} %pad_add_fusion.refs_2_, bf16[64,128,128]{2,1,0:T(8,128)(2,1)} %bitcast.55, bf16[64,128,128]{2,1,0:T(8,128)(2,1)} %bitcast.9.refs_4_, ...), custom_call_target="tpu_custom_call" | custom-call | flops 7516192768 | bytes 50000000 | tf_op jit(solution)/shard_map/units/pallas_call | solution.py:93
  (100 shorter events, 11.3 us)
Async XLA Ops:
  7.2 98.6 %collective-permute-start.27 = (bf16[5,2048,128]{1,2,0:T(8,128)(2,1)}, bf16[5,2048,128]{1,2,0:T(8,128)(2,1)S(1)}, u32[]{:S(2)}, u32[]{:S(2)}) collective-permute-start(bf16[5,2048,128]{1,2,0:T(8,128)(2,1)} %get-tuple-element.8), channel_id=1, source_target_pairs={{1,0},{2,1},{3,2},{4,3},{5,4},{6,5},{7,6},{8,7},{9,8},{10,9},{11,1... | collective-permute-start | bytes 7864328 | tf_op jit(solution)/shard_map/ppermute | solution.py:207
  15.3 10.4 %collective-permute-start.10 = (bf16[1,2,2,128,128]{4,3,2,1,0:T(8,128)(2,1)S(1)}, bf16[1,2,2,128,128]{4,3,2,1,0:T(8,128)(2,1)S(1)}, u32[]{:S(2)}, u32[]{:S(2)}) collective-permute-start(bf16[1,2,2,128,128]{4,3,2,1,0:T(8,128)(2,1)S(1)} %get-tuple-element.10), channel_id=1, source_target_pairs={{0,8},{1,9},{2,10},{3,11},{4,12},{5,13},{6,14},{7,15},{8,0},{9,1},... | collective-permute-start | bytes 393224 | tf_op jit(solution)/shard_map/ppermute | solution.py:154
  17.1 63.8 %collective-permute-start.9 = (bf16[1,2,2,128,128]{4,3,2,1,0:T(8,128)(2,1)S(1)}, bf16[1,2,2,128,128]{4,3,2,1,0:T(8,128)(2,1)S(1)}, u32[]{:S(2)}, u32[]{:S(2)}) collective-permute-start(bf16[1,2,2,128,128]{4,3,2,1,0:T(8,128)(2,1)S(1)} %get-tuple-element.10), channel_id=1, source_target_pairs={{0,12},{1,13},{2,14},{3,15},{4,0},{5,1},{6,2},{7,3},{8,4},{9,5},{1... | collective-permute-start | bytes 393224 | tf_op jit(solution)/shard_map/ppermute | solution.py:154
  23.6 58.1 %collective-permute-start.5 = (bf16[4,2,2,128,128]{4,3,2,1,0:T(8,128)(2,1)S(1)}, bf16[4,2,2,128,128]{4,3,2,1,0:T(8,128)(2,1)S(1)}, u32[]{:S(2)}, u32[]{:S(2)}) collective-permute-start(bf16[4,2,2,128,128]{4,3,2,1,0:T(8,128)(2,1)S(1)} %pad_maximum_fusion), channel_id=1, source_target_pairs={{0,4},{1,5},{2,6},{3,7},{4,8},{5,9},{6,10},{7,11},{8,12},{9,13},{1... | collective-permute-start | bytes 1572872 | tf_op jit(solution)/shard_map/ppermute | solution.py:154
  23.9 63.9 %collective-permute-start.4 = (bf16[4,2,2,128,128]{4,3,2,1,0:T(8,128)(2,1)S(1)}, bf16[4,2,2,128,128]{4,3,2,1,0:T(8,128)(2,1)S(1)}, u32[]{:S(2)}, u32[]{:S(2)}) collective-permute-start(bf16[4,2,2,128,128]{4,3,2,1,0:T(8,128)(2,1)S(1)} %pad_maximum_fusion), channel_id=1, source_target_pairs={{0,8},{1,9},{2,10},{3,11},{4,12},{5,13},{6,14},{7,15},{8,0},{9,1},... | collective-permute-start | bytes 1572872 | tf_op jit(solution)/shard_map/ppermute | solution.py:154
  25.7 61.8 %collective-permute-start.3 = (bf16[4,2,2,128,128]{4,3,2,1,0:T(8,128)(2,1)S(1)}, bf16[4,2,2,128,128]{4,3,2,1,0:T(8,128)(2,1)S(1)}, u32[]{:S(2)}, u32[]{:S(2)}) collective-permute-start(bf16[4,2,2,128,128]{4,3,2,1,0:T(8,128)(2,1)S(1)} %pad_maximum_fusion), channel_id=1, source_target_pairs={{0,12},{1,13},{2,14},{3,15},{4,0},{5,1},{6,2},{7,3},{8,4},{9,5},{1... | collective-permute-start | bytes 1572872 | tf_op jit(solution)/shard_map/ppermute | solution.py:154
  81.0 15.1 %collective-permute-start.12 = (bf16[4,2,2,128,128]{4,3,2,1,0:T(8,128)(2,1)S(1)}, bf16[4,2,2,128,128]{4,3,2,1,0:T(8,128)(2,1)S(1)}, u32[]{:S(2)}, u32[]{:S(2)}) collective-permute-start(bf16[4,2,2,128,128]{4,3,2,1,0:T(8,128)(2,1)S(1)} %pad_maximum_fusion.1), channel_id=1, source_target_pairs={{0,3},{1,0},{2,1},{3,2},{4,7},{5,4},{6,5},{7,6},{8,11},{9,8},{10,9... | collective-permute-start | bytes 1572872 | tf_op jit(solution)/shard_map/ppermute | solution.py:154
  81.8 22.3 %collective-permute-start.13 = (bf16[4,2,2,128,128]{4,3,2,1,0:T(8,128)(2,1)S(1)}, bf16[4,2,2,128,128]{4,3,2,1,0:T(8,128)(2,1)S(1)}, u32[]{:S(2)}, u32[]{:S(2)}) collective-permute-start(bf16[4,2,2,128,128]{4,3,2,1,0:T(8,128)(2,1)S(1)} %pad_maximum_fusion.1), channel_id=1, source_target_pairs={{0,2},{1,3},{2,0},{3,1},{4,6},{5,7},{6,4},{7,5},{8,10},{9,11},{10,... | collective-permute-start | bytes 1572872 | tf_op jit(solution)/shard_map/ppermute | solution.py:154
  87.5 18.0 %collective-permute-start.14 = (bf16[4,2,2,128,128]{4,3,2,1,0:T(8,128)(2,1)S(1)}, bf16[4,2,2,128,128]{4,3,2,1,0:T(8,128)(2,1)S(1)}, u32[]{:S(2)}, u32[]{:S(2)}) collective-permute-start(bf16[4,2,2,128,128]{4,3,2,1,0:T(8,128)(2,1)S(1)} %pad_maximum_fusion.1), channel_id=1, source_target_pairs={{0,1},{1,2},{2,3},{3,0},{4,5},{5,6},{6,7},{7,4},{8,9},{9,10},{10,1... | collective-permute-start | bytes 1572872 | tf_op jit(solution)/shard_map/ppermute | solution.py:154
  87.8 64.9 %collective-permute-start.26 = (bf16[5,2048,128]{1,2,0:T(8,128)(2,1)S(1)}, bf16[5,2048,128]{1,2,0:T(8,128)(2,1)S(1)}, u32[]{:S(2)}, u32[]{:S(2)}) collective-permute-start(bf16[5,2048,128]{1,2,0:T(8,128)(2,1)S(1)} %copy-done.1), channel_id=1, source_target_pairs={{0,1},{1,2},{2,3},{3,4},{4,5},{5,6},{6,7},{7,8},{8,9},{9,10},{10,1... | collective-permute-start | bytes 7864328 | tf_op jit(solution)/shard_map/ppermute | solution.py:206
  96.1 72.6 %collective-permute-start.18 = (bf16[16,2,2,128,128]{4,3,2,1,0:T(8,128)(2,1)S(1)}, bf16[16,2,2,128,128]{4,3,2,1,0:T(8,128)(2,1)S(1)}, u32[]{:S(2)}, u32[]{:S(2)}) collective-permute-start(bf16[16,2,2,128,128]{4,3,2,1,0:T(8,128)(2,1)S(1)} %constant_dynamic-update-slice_fusion), channel_id=1, source_target_pairs={{0,16},{16,0},{1,17},{17,1},{2,18},{18,2},{3,19},{19,3},{4,20},{20... | collective-permute-start | bytes 6291464 | tf_op jit(solution)/shard_map/ppermute | solution.py:157
  104.1 64.7 %collective-permute-start.7 = (bf16[16,2,2,128,128]{4,3,2,1,0:T(8,128)(2,1)S(1)}, bf16[16,2,2,128,128]{4,3,2,1,0:T(8,128)(2,1)S(1)}, u32[]{:S(2)}, u32[]{:S(2)}) collective-permute-start(bf16[16,2,2,128,128]{4,3,2,1,0:T(8,128)(2,1)S(1)} %constant_dynamic-update-slice_fusion), channel_id=1, source_target_pairs={{0,32},{1,33},{2,34},{3,35},{4,36},{5,37},{6,38},{7,39},{8,40},{9,... | collective-permute-start | bytes 6291464 | tf_op jit(solution)/shard_map/ppermute | solution.py:154
  105.5 65.3 %collective-permute-start.6 = (bf16[16,2,2,128,128]{4,3,2,1,0:T(8,128)(2,1)S(1)}, bf16[16,2,2,128,128]{4,3,2,1,0:T(8,128)(2,1)}, u32[]{:S(2)}, u32[]{:S(2)}) collective-permute-start(bf16[16,2,2,128,128]{4,3,2,1,0:T(8,128)(2,1)S(1)} %constant_dynamic-update-slice_fusion), channel_id=1, source_target_pairs={{0,96},{1,97},{2,98},{3,99},{4,100},{5,101},{6,102},{7,103},{8,104... | collective-permute-start | bytes 6291464 | tf_op jit(solution)/shard_map/ppermute | solution.py:154
  105.8 65.0 %collective-permute-start.15 = (bf16[16,2,2,128,128]{4,3,2,1,0:T(8,128)(2,1)S(1)}, bf16[16,2,2,128,128]{4,3,2,1,0:T(8,128)(2,1)}, u32[]{:S(2)}, u32[]{:S(2)}) collective-permute-start(bf16[16,2,2,128,128]{4,3,2,1,0:T(8,128)(2,1)S(1)} %constant_dynamic-update-slice_fusion.7), channel_id=1, source_target_pairs={{0,96},{1,97},{2,98},{3,99},{4,100},{5,101},{6,102},{7,103},{8,104... | collective-permute-start | bytes 6291464 | tf_op jit(solution)/shard_map/ppermute | solution.py:154
  152.8 19.7 %collective-permute-start.22 = (bf16[16,2,2,128,128]{4,3,2,1,0:T(8,128)(2,1)S(1)}, bf16[16,2,2,128,128]{4,3,2,1,0:T(8,128)(2,1)S(1)}, u32[]{:S(2)}, u32[]{:S(2)}) collective-permute-start(bf16[16,2,2,128,128]{4,3,2,1,0:T(8,128)(2,1)S(1)} %constant_dynamic-update-slice_fusion.7), channel_id=1, source_target_pairs={{0,16},{16,0},{1,17},{17,1},{2,18},{18,2},{3,19},{19,3},{4,20},{20... | collective-permute-start | bytes 6291464 | tf_op jit(solution)/shard_map/ppermute | solution.py:157
  168.7 45.7 %collective-permute-start.17 = (bf16[16,2,2,128,128]{4,3,2,1,0:T(8,128)(2,1)S(1)}, bf16[16,2,2,128,128]{4,3,2,1,0:T(8,128)(2,1)S(1)}, u32[]{:S(2)}, u32[]{:S(2)}) collective-permute-start(bf16[16,2,2,128,128]{4,3,2,1,0:T(8,128)(2,1)S(1)} %constant_dynamic-update-slice_fusion.7), channel_id=1, source_target_pairs={{0,32},{1,33},{2,34},{3,35},{4,36},{5,37},{6,38},{7,39},{8,40},{9,... | collective-permute-start | bytes 6291464 | tf_op jit(solution)/shard_map/ppermute | solution.py:154
  168.8 45.7 %collective-permute-start.21 = (bf16[16,2,2,128,128]{4,3,2,1,0:T(8,128)(2,1)S(1)}, bf16[16,2,2,128,128]{4,3,2,1,0:T(8,128)(2,1)S(1)}, u32[]{:S(2)}, u32[]{:S(2)}) collective-permute-start(bf16[16,2,2,128,128]{4,3,2,1,0:T(8,128)(2,1)S(1)} %collective-permute-done.7), channel_id=1, source_target_pairs={{0,16},{16,0},{1,17},{17,1},{2,18},{18,2},{3,19},{19,3},{4,20},{20... | collective-permute-start | bytes 6291464 | tf_op jit(solution)/shard_map/ppermute | solution.py:157
  170.8 45.7 %collective-permute-start.8 = (bf16[16,2,2,128,128]{4,3,2,1,0:T(8,128)(2,1)S(1)}, bf16[16,2,2,128,128]{4,3,2,1,0:T(8,128)(2,1)}, u32[]{:S(2)}, u32[]{:S(2)}) collective-permute-start(bf16[16,2,2,128,128]{4,3,2,1,0:T(8,128)(2,1)S(1)} %collective-permute-done.7), channel_id=1, source_target_pairs={{0,32},{1,33},{2,34},{3,35},{4,36},{5,37},{6,38},{7,39},{8,40},{9,... | collective-permute-start | bytes 6291464 | tf_op jit(solution)/shard_map/ppermute | solution.py:154
  170.9 48.0 %collective-permute-start.16 = (bf16[16,2,2,128,128]{4,3,2,1,0:T(8,128)(2,1)}, bf16[16,2,2,128,128]{4,3,2,1,0:T(8,128)(2,1)}, u32[]{:S(2)}, u32[]{:S(2)}) collective-permute-start(bf16[16,2,2,128,128]{4,3,2,1,0:T(8,128)(2,1)} %collective-permute-done.15), channel_id=1, source_target_pairs={{0,96},{1,97},{2,98},{3,99},{4,100},{5,101},{6,102},{7,103},{8,104... | collective-permute-start | bytes 6291464 | tf_op jit(solution)/shard_map/ppermute | solution.py:154
  172.5 72.3 %collective-permute-start.23 = (bf16[16,2,2,128,128]{4,3,2,1,0:T(8,128)(2,1)}, bf16[16,2,2,128,128]{4,3,2,1,0:T(8,128)(2,1)}, u32[]{:S(2)}, u32[]{:S(2)}) collective-permute-start(bf16[16,2,2,128,128]{4,3,2,1,0:T(8,128)(2,1)} %collective-permute-done.15), channel_id=1, source_target_pairs={{0,16},{16,0},{1,17},{17,1},{2,18},{18,2},{3,19},{19,3},{4,20},{20... | collective-permute-start | bytes 6291464 | tf_op jit(solution)/shard_map/ppermute | solution.py:157
  214.4 30.3 %collective-permute-start.19 = (bf16[16,2,2,128,128]{4,3,2,1,0:T(8,128)(2,1)}, bf16[16,2,2,128,128]{4,3,2,1,0:T(8,128)(2,1)}, u32[]{:S(2)}, u32[]{:S(2)}) collective-permute-start(bf16[16,2,2,128,128]{4,3,2,1,0:T(8,128)(2,1)} %collective-permute-done.6), channel_id=1, source_target_pairs={{0,16},{16,0},{1,17},{17,1},{2,18},{18,2},{3,19},{19,3},{4,20},{20... | collective-permute-start | bytes 6291464 | tf_op jit(solution)/shard_map/ppermute | solution.py:157
  214.5 30.2 %collective-permute-start.25 = (bf16[16,2,2,128,128]{4,3,2,1,0:T(8,128)(2,1)S(1)}, bf16[16,2,2,128,128]{4,3,2,1,0:T(8,128)(2,1)}, u32[]{:S(2)}, u32[]{:S(2)}) collective-permute-start(bf16[16,2,2,128,128]{4,3,2,1,0:T(8,128)(2,1)S(1)} %collective-permute-done.17), channel_id=1, source_target_pairs={{0,16},{16,0},{1,17},{17,1},{2,18},{18,2},{3,19},{19,3},{4,20},{20... | collective-permute-start | bytes 6291464 | tf_op jit(solution)/shard_map/ppermute | solution.py:157
  216.5 28.2 %collective-permute-start.20 = (bf16[16,2,2,128,128]{4,3,2,1,0:T(8,128)(2,1)}, bf16[16,2,2,128,128]{4,3,2,1,0:T(8,128)(2,1)}, u32[]{:S(2)}, u32[]{:S(2)}) collective-permute-start(bf16[16,2,2,128,128]{4,3,2,1,0:T(8,128)(2,1)} %collective-permute-done.8), channel_id=1, source_target_pairs={{0,16},{16,0},{1,17},{17,1},{2,18},{18,2},{3,19},{19,3},{4,20},{20... | collective-permute-start | bytes 6291464 | tf_op jit(solution)/shard_map/ppermute | solution.py:157
  218.9 26.9 %collective-permute-start.24 = (bf16[16,2,2,128,128]{4,3,2,1,0:T(8,128)(2,1)}, bf16[16,2,2,128,128]{4,3,2,1,0:T(8,128)(2,1)}, u32[]{:S(2)}, u32[]{:S(2)}) collective-permute-start(bf16[16,2,2,128,128]{4,3,2,1,0:T(8,128)(2,1)} %collective-permute-done.16), channel_id=1, source_target_pairs={{0,16},{16,0},{1,17},{17,1},{2,18},{18,2},{3,19},{19,3},{4,20},{20... | collective-permute-start | bytes 6291464 | tf_op jit(solution)/shard_map/ppermute | solution.py:157
  (18 other events, 753.5 us)
